TPU v7x, 32 devices: a whole 2x2x4 slice. The times are simulated.
32 devices in a mesh: pts: 8 (over z, y), hrs: 4 (over x, core).
Axes of the slice: x: 2, y: 2, z: 4, core: 2. Of those that a mesh axis runs over, the one named last changes fastest.
Arguments:
- fields: float32 [512, 65536], P(('pts', 'hrs')), may hold values from -2000 to 2000, as said below
- probes: float32 [256, 512], replicated, may hold values from -0.25 to 0.25
Outputs:
- basis_rows: float32 [256, 65536], P(None, ('pts', 'hrs'))
- coeffs: float32 [256, 512], replicated
Inputs may be any that keep to these rules, and one draw needn't show every extreme that they name: `fields`: every hour and every grid point carries its own scale, and the values are real-valued and never all zero.
All inputs are finite; a program needn't handle non-finite values.
Results may differ from a plain program's by a relative error of at most 0.00017.
Values sent between devices are 32-bit elements; how exact they have to be, the bound alone decides.
A program may use at most 64 MiB of HBM per device.

v0:
```python
import jax
import jax.numpy as jnp
from jax import lax
from jax.sharding import PartitionSpec as P

highest = lax.Precision.HIGHEST


def contract_last(left, right):
    return lax.dot_general(
        left, right, (((1,), (1,)), ((), ())), precision=highest, preferred_element_type=jnp.float32
    )


def on_device(fields, probes):
    n_pts = lax.axis_size("pts")
    n_hrs = lax.axis_size("hrs")
    panels = lax.all_to_all(fields, ("pts", "hrs"), split_axis=1, concat_axis=0, tiled=True)
    n_points = panels.shape[1] * n_pts * n_hrs
    sketched = jnp.dot(probes, panels, precision=highest, preferred_element_type=jnp.float32)
    cross_sum = lax.psum(contract_last(sketched, panels) / n_points, ("pts", "hrs"))
    local_gram = contract_last(sketched, sketched) / n_points
    gram_sum = lax.psum(local_gram, ("pts", "hrs"))
    factor = jnp.linalg.cholesky(gram_sum)
    basis_rows = lax.linalg.triangular_solve(factor, sketched, left_side=True, lower=True)
    coeffs = lax.linalg.triangular_solve(factor, cross_sum, left_side=True, lower=True)
    return (basis_rows, coeffs)


def solution(mesh):
    return jax.shard_map(
        on_device,
        mesh=mesh,
        in_specs=(P(("pts", "hrs"), None), P()),
        out_specs=(P(None, ("pts", "hrs")), P()),
        check_vma=False,
    )
```

profile of v0, /device:TPU:0, one launch (start us, length us, event | category | flops | bytes accessed | tf_op | source)
XLA Modules:
  0.0 328.4 jit_solution(12238962326394786213)
XLA Ops:
  7.2 0.0 copy-start
  7.2 0.0 all-reduce.4.cloned.1.call-start
  7.2 2.5 copy.17
  9.7 100.7 %all_to_all.19 = f32[16,32,2048]{2,0,1:T(8,128)S(1)} all-to-all(f32[16,32,2048]{2,0,1:T(8,128)S(1)} %bitcast.50), channel_id=1, replica_groups=mesh['pts'=8,'hrs'=4] {'pts','hrs'}, dimensions={1} | all-to-all | bytes 8388608 | tf_op jit(solution)/shard_map/all_to_all | solution.py:18
  110.5 0.0 copy-done
  110.5 3.7 %fusion.13 = f32[256,2048]{1,0:T(8,128)S(1)} fusion(f32[256,512]{1,0:T(8,128)S(1)} %copy-done, f32[512,2048]{1,0:T(8,128)S(1)} %bitcast.48), kind=kOutput, calls=%fused_computation.38 | convolution fusion | flops 3221225472 | bytes 6815744 | tf_op jit(solution)/shard_map/dot_general | solution.py:20
  114.2 4.5 %convolution_multiply_fusion = f32[256,512]{1,0:T(8,128)} fusion(f32[256,2048]{1,0:T(8,128)S(1)} %fusion.13, f32[512,2048]{1,0:T(8,128)S(1)} %bitcast.49), kind=kOutput, calls=%fused_computation.5 | convolution fusion | flops 3221356544 | bytes 6815744 | tf_op jit(solution)/shard_map/dot_general | solution.py:10
  118.7 2.6 convolution_multiply_fusion.1
  121.3 0.0 all-reduce.4.cloned.1.call-update
  121.3 129.5 %all-reduce.4.cloned.1.call-done = (f32[256,256]{0,1:T(8,128)}, f32[256,512]{1,0:T(8,128)}) async-done(((f32[256,256]{0,1:T(8,128)}, f32[256,512]{1,0:T(8,128)}), (f32[256,256]{0,1:T(8,128)}, f32[256,512]{1,0:T(8,128)})) %all-reduce.4.cloned.1.call-update) | async-done | bytes 786448 | tf_op jit(solution)/shard_map/psum | solution.py:23
  250.9 1.1 copy.13
  252.0 1.0 fusion.4
  253.0 11.9 %cholesky.50 = f32[128,128]{1,0:T(8,128)S(1)} custom-call(f32[128,128]{1,0:T(8,128)S(1)} %cholesky.118), custom_call_target="Cholesky" | custom-call | tf_op jit(solution)/shard_map/jit(cholesky)/cholesky | solution.py:24
  264.9 9.8 %custom-call.16 = f32[1,128,128]{1,2,0:T(8,128)S(1)} custom-call(f32[1,128,128]{2,1,0:T(8,128)S(1)} %get-tuple-element.25), custom_call_target="InvertDiagBlocksLowerTriangular" | custom-call | tf_op jit(solution)/shard_map/jit(cholesky)/cholesky | solution.py:24
  274.7 0.2 constant_dynamic-update-slice_fusion.1
  274.9 0.3 convolution_subtract_fusion.2
  275.2 11.7 %cholesky.105 = f32[128,128]{1,0:T(8,128)S(1)} custom-call(f32[128,128]{1,0:T(8,128)S(1)} %convolution_subtract_fusion.2), custom_call_target="Cholesky" | custom-call | tf_op jit(solution)/shard_map/jit(cholesky)/cholesky | solution.py:24
  287.0 0.6 compare_reduce_fusion
  288.9 0.1 triangular_solve.72
  289.0 4.0 %while.1 = (s32[]{:T(128)}, f32[256,256]{1,0:T(8,128)S(1)}, s32[2,2]{1,0:T(2,128)S(1)}, f32[2,128,128]{2,1,0:T(8,128)S(1)}, s32[]{:T(128)}) while((s32[]{:T(128)}, f32[256,256]{1,0:T(8,128)S(1)}, s32[2,2]{1,0:T(2,128)S(1)}, f32[2,128,128]{2,1,0:T(8,128)S(1)}, s32[]{:T(128)}) %tuple.27), condition=%wide.while_cond, body=%wide.while_body.sunk | while | flops 2 | bytes 131181 | solution.py:25
  289.0 0.6 fusion.27
  289.6 1.4 bitcast_dynamic-update-slice_fusion.2
  291.0 0.6 fusion.27
  291.6 1.4 bitcast_dynamic-update-slice_fusion.2
  293.0 19.9 %custom-call.17 = f32[2,128,128]{1,2,0:T(8,128)S(1)} custom-call(f32[2,128,128]{2,1,0:T(8,128)S(1)} %get-tuple-element.9), custom_call_target="InvertDiagBlocksLowerTriangular" | custom-call | tf_op jit(solution)/shard_map/triangular_solve | solution.py:25
  312.9 1.1 fusion
  314.0 1.4 fusion.2
  315.3 1.3 convolution_subtract_fusion.1
  316.7 0.4 fusion.8
  317.1 0.8 pad_maximum_fusion.1
  317.9 1.0 convolution_subtract_fusion
  319.0 1.0 fusion.9
  320.0 1.5 pad_maximum_fusion
  (9 shorter events, 0.1 us)
Async XLA Ops:
  7.2 103.3 %copy-start = (f32[256,512]{1,0:T(8,128)S(1)}, f32[256,512]{1,0:T(8,128)}, u32[]{:S(2)}) copy-start(f32[256,512]{1,0:T(8,128)} %param.3) | copy-start | bytes 1572868
  7.2 243.7 %all-reduce.4.cloned.1.call-start = ((), (), s32[]{:S(2)}) async-start(), calls=%async_computation.1 | async-start | bytes 1572864 | tf_op jit(solution)/shard_map/psum | solution.py:23
Sparse Core Ops, SparseCore 0:
  121.4 129.3 all-reduce.3
where the time goes:
time: 329 us; the launch traced here: 328 us
  waiting for transfers between devices  130 us (40%)
  blocking collectives  101 us (31%)
  other arithmetic  57.4 us (17%)
  matrix products  17.5 us (5%)
  between operations  15.5 us (5%)
  local copies, waits for them, and re-layouts  7.64 us (2%)
    psum x1, waiting for transfers between devices, on_device(): gram_sum = lax.psum(local_gram, ('pts', 'hrs'))  130 us
    all_to_all x1, blocking collectives, on_device(): lax.all_to_all(fields, ('pts', 'hrs'), split_axis=1, concat_axis=0, tiled...  101 us
    another operation x6, other arithmetic, on_device(): factor = jnp.linalg.cholesky(gram_sum)  34.1 us
    another operation x4, other arithmetic, on_device(): lax.linalg.triangular_solve(factor, sketched, left_side=True, lower=True)  21.5 us
    dot_general x2, matrix products, contract_last(): lax.dot_general(left, right, (((1,), (1,)), ((), ())), precision=highest,...  7.09 us
  transfers between devices with their start and end apart: 1, of which 1 were waited for; matrix products, arithmetic and copies ran while one was open for 0% of the time, Pallas kernels for 0%

commit v1 on v0

v1 whole, which is shorter than its diff:
```python
import functools

import jax
import jax.numpy as jnp
from jax import lax
from jax.experimental import pallas as pl
from jax.experimental.pallas import tpu as pltpu
from jax.sharding import PartitionSpec as P

HI = lax.Precision.HIGHEST

def mm(a, b, dims):
    return lax.dot_general(a, b, (dims, ((), ())), precision=HI, preferred_element_type=jnp.float32)

def invert_block(block):
    b = block.shape[0]
    rows = lax.broadcasted_iota(jnp.int32, (b, 2 * b), 0)
    cols = lax.broadcasted_iota(jnp.int32, (b, 2 * b), 1)
    eye = (rows + b == cols).astype(jnp.float32)
    m = jnp.concatenate([block, eye[:, b:]], axis=1)
    strips = [m[8 * s:8 * s + 8] for s in range(b // 8)]
    srow = lax.broadcasted_iota(jnp.int32, (8, 2 * b), 0)
    for j in range(b - 1):
        s0, r = divmod(j, 8)
        pivot = strips[s0][r:r + 1, :]
        inv = 1.0 / pivot[:, j:j + 1]
        scaled = pivot * inv
        for s in range(s0, b // 8):
            f = strips[s][:, j:j + 1]
            if s == s0:
                if r == 7:
                    continue
                f = jnp.where(srow[:, :1] > r, f, 0.0)
            strips[s] = strips[s] - f * scaled
    m = jnp.concatenate(strips, axis=0)
    d = jnp.sum(jnp.where(rows == cols, m, 0.0), axis=1, keepdims=True)
    return m[:, b:] * lax.rsqrt(d)

def factor_kernel(cross_ref, probes_ref, sk_ref, basis_ref, coeffs_ref, aug, winv):
    k = cross_ref.shape[0]
    b = 64
    aug[:, :k] = mm(cross_ref[...], probes_ref[...], ((1,), (1,)))
    rows = lax.broadcasted_iota(jnp.int32, (k, k), 0)
    cols = lax.broadcasted_iota(jnp.int32, (k, k), 1)
    aug[:, k:] = (rows == cols).astype(jnp.float32)
    for i in range(k // b):
        lo, hi = i * b, (i + 1) * b
        w = invert_block(aug[lo:hi, lo:hi])
        done = mm(w, aug[lo:hi, :], ((1,), (0,)))
        winv[lo:hi, :] = done[:, k:]
        if hi < k:
            aug[hi:, :] = aug[hi:, :] - mm(done[:, hi:k], done, ((0,), (0,)))
    w = winv[...]
    coeffs_ref[...] = mm(w, cross_ref[...], ((1,), (0,)))
    n = sk_ref.shape[1]
    @pl.loop(0, n // 512)
    def _(t):
        c = pl.ds(pl.multiple_of(t * 512, 512), 512)
        basis_ref[:, c] = mm(w, sk_ref[:, c], ((1,), (0,)))

def finish(cross, probes, sk):
    k = cross.shape[0]
    v = pl.BlockSpec(memory_space=pltpu.VMEM)
    return pl.pallas_call(factor_kernel,
        out_shape=(jax.ShapeDtypeStruct(sk.shape, jnp.float32), jax.ShapeDtypeStruct(cross.shape, jnp.float32)),
        in_specs=[v, v, v], out_specs=(v, v),
        scratch_shapes=[pltpu.VMEM((k, 2 * k), jnp.float32), pltpu.VMEM((k, k), jnp.float32)],
        name="factor")(cross, probes, sk)


def sum_kernel(n_pts, n_hrs, x_ref, out_ref, got1, part, got2, s1, r1, s2, r2, s3, r3, s4, r4):
    pts, hrs = lax.axis_index("pts"), lax.axis_index("hrs")
    rows, width = x_ref.shape
    q = rows // n_hrs
    cols = q * width // (8 * n_pts)
    per_row = width // cols

    def peer_hrs(o):
        return lax.rem(hrs + o, n_hrs)

    def peer_pts(o):
        return lax.rem(pts + o, n_pts)

    def tile(p):
        return (
            pl.ds(pl.multiple_of((p // per_row) * 8, 8), 8),
            pl.ds(pl.multiple_of(lax.rem(p, per_row) * cols, 128), cols),
        )

    barrier = pltpu.get_barrier_semaphore()
    for o in range(1, n_hrs):
        pl.semaphore_signal(barrier, inc=1, device_id=(pts, peer_hrs(o)), device_id_type=pl.DeviceIdType.MESH)
    for o in range(1, n_pts):
        pl.semaphore_signal(barrier, inc=1, device_id=(peer_pts(o), hrs), device_id_type=pl.DeviceIdType.MESH)
    pl.semaphore_wait(barrier, n_hrs + n_pts - 2)

    def send(src, dst, ss, rs, device):
        copy = pltpu.make_async_remote_copy(
            src_ref=src, dst_ref=dst, send_sem=ss, recv_sem=rs,
            device_id=device, device_id_type=pl.DeviceIdType.MESH,
        )
        copy.start()
        return copy

    mine = pl.ds(pl.multiple_of(hrs * q, 8), q)
    copies = []
    for o in range(1, n_hrs):
        t = peer_hrs(o)
        src = x_ref.at[pl.ds(pl.multiple_of(t * q, 8), q)]
        copies.append(send(src, got1.at[o - 1], s1.at[o - 1], r1.at[o - 1], (pts, t)))
    total = x_ref[mine, :]
    for o, copy in enumerate(copies):
        copy.wait_recv()
        total = total + got1[o]
    part[...] = total

    copies2 = []
    for o in range(1, n_pts):
        t = peer_pts(o)
        copies2.append(send(part.at[tile(t)], got2.at[o - 1], s2.at[o - 1], r2.at[o - 1], (t, hrs)))
    total = part[tile(pts)]
    for o, copy in enumerate(copies2):
        copy.wait_recv()
        total = total + got2[o]
    tr, tc = tile(pts)
    own = (pl.ds(pl.multiple_of(hrs * q + (pts // per_row) * 8, 8), 8), tc)
    out_ref[own] = total

    copies3 = []
    for o in range(1, n_pts):
        t = peer_pts(o)
        copies3.append(send(out_ref.at[own], out_ref.at[own], s3.at[o - 1], r3.at[o - 1], (t, hrs)))
    for copy in copies3:
        copy.wait_recv()
    copies4 = []
    for o in range(1, n_hrs):
        t = peer_hrs(o)
        copies4.append(send(out_ref.at[mine], out_ref.at[mine], s4.at[o - 1], r4.at[o - 1], (pts, t)))
    for copy in copies4:
        copy.wait_recv()
    for copy in copies + copies2 + copies3 + copies4:
        copy.wait_send()


def sum_all(x, n_pts, n_hrs):
    rows, width = x.shape
    q = rows // n_hrs
    cols = q * width // (8 * n_pts)
    v = pl.BlockSpec(memory_space=pltpu.VMEM)
    dma = pltpu.SemaphoreType.DMA
    return pl.pallas_call(
        functools.partial(sum_kernel, n_pts, n_hrs),
        out_shape=jax.ShapeDtypeStruct(x.shape, jnp.float32),
        in_specs=[v],
        out_specs=v,
        scratch_shapes=[
            pltpu.VMEM((n_hrs - 1, q, width), jnp.float32),
            pltpu.VMEM((q, width), jnp.float32),
            pltpu.VMEM((n_pts - 1, 8, cols), jnp.float32),
            dma((n_hrs - 1,)), dma((n_hrs - 1,)),
            dma((n_pts - 1,)), dma((n_pts - 1,)),
            dma((n_pts - 1,)), dma((n_pts - 1,)),
            dma((n_hrs - 1,)), dma((n_hrs - 1,)),
        ],
        compiler_params=pltpu.CompilerParams(collective_id=0, has_side_effects=True),
        name="sum_all",
    )(x)


def on_device(fields, probes):
    n_pts = lax.axis_size("pts")
    n_hrs = lax.axis_size("hrs")
    panels = lax.all_to_all(fields, ("pts", "hrs"), split_axis=1, concat_axis=0, tiled=True)
    n_points = panels.shape[1] * n_pts * n_hrs
    sketched = jnp.dot(probes, panels, precision=HI, preferred_element_type=jnp.float32)
    cross = sum_all(mm(sketched, panels, ((1,), (1,))) / n_points, n_pts, n_hrs)
    return finish(cross, probes, sketched)


def solution(mesh):
    return jax.shard_map(
        on_device,
        mesh=mesh,
        in_specs=(P(("pts", "hrs"), None), P()),
        out_specs=(P(None, ("pts", "hrs")), P()),
        check_vma=False,
    )
```

time: 329 us -> 170 us (0.52)
  waiting for transfers between devices: 130 us -> 0 us
  other arithmetic: 57.4 us -> 0 us
  Pallas kernels: 0 us -> 56.8 us
  between operations: 15.5 us -> 0.67 us
  matrix products: 17.5 us -> 8.23 us
  local copies, waits for them, and re-layouts: 7.64 us -> 2.47 us
    psum x1 -> x0, waiting for transfers between devices: 130 us -> none  [on_device(): gram_sum = lax.psum(local_gram, ('pts', 'hrs'))]
    pallas_call x0 -> x2, Pallas kernels: none -> 56.8 us  [the longest x1 30.8 us: finish(): pl.pallas_call(factor_kernel, out_shape=(jax.ShapeDtypeStruct(sk.shape, j...]
    another operation x11 -> x0, other arithmetic: 56.4 us -> none  [the longest x6 34.1 us: on_device(): factor = jnp.linalg.cholesky(gram_sum)]
    another operation x8 -> x0, matrix products: 6.69 us -> none  [the longest x3 3.11 us: on_device(): lax.linalg.triangular_solve(factor, cross_sum, left_side=True, lower=True)]
    another operation x9 -> x0, local copies, waits for them, and re-layouts: 4.05 us -> none
    dot_general x3 -> x2, matrix products: 10.8 us -> 8.23 us  [the longest x1 4.52 us: mm(): lax.dot_general(a, b, (dims, ((), ())), precision=HI, preferred_element_t...]
  transfers between devices with their start and end apart: 1 -> 0, of which waited for: 1 -> 0; matrix products, arithmetic and copies ran while one was open for 0% -> 0% of each run, Pallas kernels for 0% -> 0%
where the time goes in v1:
time: 170 us; the launch traced here: 169 us
  blocking collectives  101 us (59%)
  Pallas kernels  56.8 us (33%)
  matrix products  8.23 us (5%)
  local copies, waits for them, and re-layouts  2.47 us (1%)
    all_to_all x1, blocking collectives, on_device(): lax.all_to_all(fields, ('pts', 'hrs'), split_axis=1, concat_axis=0, tiled...  101 us
    pallas_call x1, Pallas kernels, finish(): pl.pallas_call(factor_kernel, out_shape=(jax.ShapeDtypeStruct(sk.shape, j...  30.8 us
    pallas_call x1, Pallas kernels, sum_all(): pl.pallas_call(functools.partial(sum_kernel, n_pts, n_hrs), out_shape=jax...  26 us
    dot_general x1, matrix products, mm(): lax.dot_general(a, b, (dims, ((), ())), precision=HI, preferred_element_t...  4.52 us
    dot_general x1, matrix products, on_device(): jnp.dot(probes, panels, precision=HI, preferred_element_type=jnp.float32)  3.71 us

profile of v1, /device:TPU:0, one launch (start us, length us, event | category | flops | bytes accessed | tf_op | source)
XLA Modules:
  0.0 169.0 jit_solution(11771991866365385885)
XLA Ops:
  0.6 2.5 %copy.8 = f32[2,32,8,2048]{3,2,0,1:T(8,128)S(1)} copy(f32[2,32,8,2048]{3,2,1,0:T(8,128)} %bitcast.14) | data formatting | bytes 8388608 | tf_op jit(solution)/shard_map/all_to_all | solution.py:173
  3.1 0.0 copy-start.1
  3.1 100.7 %all_to_all.19 = f32[16,32,2048]{2,0,1:T(8,128)S(1)} all-to-all(f32[16,32,2048]{2,0,1:T(8,128)S(1)} %bitcast.13), channel_id=1, replica_groups=mesh['pts'=8,'hrs'=4] {'pts','hrs'}, dimensions={1} | all-to-all | bytes 8388608 | tf_op jit(solution)/shard_map/all_to_all | solution.py:173
  103.9 0.0 copy-done.1
  103.9 3.7 %fusion.sk_ref = f32[256,2048]{1,0:T(8,128)S(1)} fusion(f32[256,512]{1,0:T(8,128)S(1)} %copy-done.1, f32[512,2048]{1,0:T(8,128)S(1)} %bitcast.11), kind=kOutput, calls=%fused_computation.2 | convolution fusion | flops 3221225472 | bytes 6815744 | tf_op jit(solution)/shard_map/dot_general | solution.py:175
  107.6 0.0 copy-start
  107.6 4.5 %convolution_multiply_fusion.x_ref = f32[256,512]{1,0:T(8,128)} fusion(f32[256,2048]{1,0:T(8,128)S(1)} %fusion.sk_ref, f32[512,2048]{1,0:T(8,128)S(1)} %bitcast.12), kind=kOutput, calls=%fused_computation.1 | convolution fusion | flops 3221356544 | bytes 6815744 | tf_op jit(solution)/shard_map/dot_general | solution.py:13
  112.1 26.0 %sum_all.1.cross_ref = f32[256,512]{1,0:T(8,128)} custom-call(f32[256,512]{1,0:T(8,128)} %convolution_multiply_fusion.x_ref), custom_call_target="tpu_custom_call" | custom-call | tf_op jit(solution)/shard_map/sum_all/pallas_call | solution.py:151
  138.1 0.0 copy-done
  138.1 30.8 %factor.1 = (f32[256,2048]{1,0:T(8,128)}, f32[256,512]{1,0:T(8,128)}) custom-call(f32[256,512]{1,0:T(8,128)} %sum_all.1.cross_ref, f32[256,512]{1,0:T(8,128)} %probes_ref.1, f32[256,2048]{1,0:T(8,128)} %copy-done), custom_call_target="tpu_custom_call" | custom-call | tf_op jit(solution)/shard_map/factor/pallas_call | solution.py:64
Async XLA Ops:
  3.1 100.8 %copy-start.1 = (f32[256,512]{1,0:T(8,128)S(1)}, f32[256,512]{1,0:T(8,128)}, u32[]{:S(2)}) copy-start(f32[256,512]{1,0:T(8,128)} %probes_ref.1) | copy-start | bytes 1572868
  107.6 30.5 %copy-start = (f32[256,2048]{1,0:T(8,128)}, f32[256,2048]{1,0:T(8,128)S(1)}, u32[]{:S(2)}) copy-start(f32[256,2048]{1,0:T(8,128)S(1)} %fusion.sk_ref) | copy-start | bytes 6291460

commit v2 on v1

--- a/solution.py
+++ b/solution.py
@@ -167,14 +167,92 @@
     )(x)
 
 
+def gather_kernel(n_pts, n_hrs, chunks, n_points, fields_ref, probes_ref, sk_ref, cross_ref, panels, flat, own_sem, send_sem, recv_sem):
+    pts, hrs = lax.axis_index("pts"), lax.axis_index("hrs")
+    n = n_pts * n_hrs
+    me = pts * n_hrs + hrs
+    rows = fields_ref.shape[0]
+    width = panels.shape[3]
+    local = width * chunks
+
+    def split(o):
+        t = lax.rem(me + o, n)
+        return t, t // n_hrs, lax.rem(t, n_hrs)
+
+    barrier = pltpu.get_barrier_semaphore()
+
+    @pl.loop(1, n)
+    def _(o):
+        _, tp, th = split(o)
+        pl.semaphore_signal(barrier, inc=1, device_id=(tp, th), device_id_type=pl.DeviceIdType.MESH)
+
+    pl.semaphore_wait(barrier, n - 1)
+
+    def source(t, c):
+        return fields_ref.at[:, pl.ds(pl.multiple_of(t * local + c * width, 128), width)]
+
+    owns = []
+    for c in range(chunks):
+        @pl.loop(1, n)
+        def _(o):
+            t, tp, th = split(o)
+            pltpu.make_async_remote_copy(
+                src_ref=source(t, c), dst_ref=panels.at[c, me], send_sem=send_sem.at[c], recv_sem=recv_sem.at[c],
+                device_id=(tp, th), device_id_type=pl.DeviceIdType.MESH,
+            ).start()
+
+        own = pltpu.make_async_copy(source(me, c), panels.at[c, me], own_sem.at[c])
+        own.start()
+        owns.append(own)
+
+    for c in range(chunks):
+        owns[c].wait()
+        most = panels.at[c, pl.ds(0, n - 1)]
+        pltpu.make_async_copy(most, most, recv_sem.at[c]).wait()
+        if rows % 8 == 0:
+            block = panels[c].reshape(n * rows, width)
+        else:
+            for d in range(n):
+                flat[d * rows:(d + 1) * rows, :] = panels[c, d]
+            block = flat[...]
+        sk = mm(probes_ref[...], block, ((1,), (0,)))
+        sk_ref[:, c * width:(c + 1) * width] = sk
+        term = mm(sk, block, ((1,), (1,)))
+        cross_ref[...] = term if c == 0 else cross_ref[...] + term
+    cross_ref[...] = cross_ref[...] / n_points
+    for c in range(chunks):
+        most = panels.at[c, pl.ds(0, n - 1)]
+        pltpu.make_async_copy(most, most, send_sem.at[c]).wait()
+
+
+def gather(fields, probes, n_pts, n_hrs, chunks):
+    k, hours = probes.shape
+    rows, n_points = fields.shape
+    n = n_pts * n_hrs
+    local = n_points // n
+    width = local // chunks
+    v = pl.BlockSpec(memory_space=pltpu.VMEM)
+    dma = pltpu.SemaphoreType.DMA
+    return pl.pallas_call(
+        functools.partial(gather_kernel, n_pts, n_hrs, chunks, n_points),
+        out_shape=(jax.ShapeDtypeStruct((k, local), jnp.float32), jax.ShapeDtypeStruct((k, hours), jnp.float32)),
+        in_specs=[pl.BlockSpec(memory_space=pl.ANY), v],
+        out_specs=(v, v),
+        scratch_shapes=[
+            pltpu.VMEM((chunks, n, rows, width), jnp.float32),
+            pltpu.VMEM((hours, width) if rows % 8 else (8, 128), jnp.float32),
+            dma((chunks,)), dma((chunks,)), dma((chunks,)),
+        ],
+        compiler_params=pltpu.CompilerParams(collective_id=1, has_side_effects=True),
+        name="gather",
+    )(fields, probes)
+
+
 def on_device(fields, probes):
     n_pts = lax.axis_size("pts")
     n_hrs = lax.axis_size("hrs")
-    panels = lax.all_to_all(fields, ("pts", "hrs"), split_axis=1, concat_axis=0, tiled=True)
-    n_points = panels.shape[1] * n_pts * n_hrs
-    sketched = jnp.dot(probes, panels, precision=HI, preferred_element_type=jnp.float32)
-    cross = sum_all(mm(sketched, panels, ((1,), (1,))) / n_points, n_pts, n_hrs)
-    return finish(cross, probes, sketched)
+    sketched, cross = gather(fields, probes, n_pts, n_hrs, 4)
+    return finish(sum_all(cross, n_pts, n_hrs), probes, sketched)
 
 
 def solution(mesh):

time: 170 us -> 162 us (0.953)
  Pallas kernels: 56.8 us -> 161 us
  blocking collectives: 101 us -> 0 us
  matrix products: 8.23 us -> 0 us
  local copies, waits for them, and re-layouts: 2.47 us -> 0 us
    all_to_all x1 -> x0, blocking collectives: 101 us -> none  [on_device(): lax.all_to_all(fields, ('pts', 'hrs'), split_axis=1, concat_axis=0, tiled...]
    pallas_call x0 -> x1, Pallas kernels: none -> 94.5 us  [gather(): pl.pallas_call(functools.partial(gather_kernel, n_pts, n_hrs, chunks, n_p...]
    pallas_call x1, Pallas kernels: 26 us -> 35.8 us  [sum_all(): pl.pallas_call(functools.partial(sum_kernel, n_pts, n_hrs), out_shape=jax...]
    dot_general x2 -> x0, matrix products: 8.23 us -> none  [the longest x1 4.52 us: mm(): lax.dot_general(a, b, (dims, ((), ())), precision=HI, preferred_element_t...]
    all_to_all x1 -> x0, local copies, waits for them, and re-layouts: 2.46 us -> none  [on_device(): lax.all_to_all(fields, ('pts', 'hrs'), split_axis=1, concat_axis=0, tiled...]
where the time goes in v2:
time: 162 us
  Pallas kernels  161 us (99%)
    pallas_call x1, Pallas kernels, gather(): pl.pallas_call(functools.partial(gather_kernel, n_pts, n_hrs, chunks, n_p...  94.5 us
    pallas_call x1, Pallas kernels, sum_all(): pl.pallas_call(functools.partial(sum_kernel, n_pts, n_hrs), out_shape=jax...  35.8 us
    pallas_call x1, Pallas kernels, finish(): pl.pallas_call(factor_kernel, out_shape=(jax.ShapeDtypeStruct(sk.shape, j...  30.7 us

profile of v2, /device:TPU:0, one launch (start us, length us, event | category | flops | bytes accessed | tf_op | source)
XLA Modules:
  0.0 161.7 jit_solution(6053414043855437890)
XLA Ops:
  0.6 94.5 %gather.1 = (f32[256,2048]{1,0:T(8,128)}, f32[256,512]{1,0:T(8,128)}) custom-call(f32[16,65536]{1,0:T(8,128)} %fields_ref.1, f32[256,512]{1,0:T(8,128)} %probes_ref.3), custom_call_target="tpu_custom_call" | custom-call | tf_op jit(solution)/shard_map/gather/pallas_call | solution.py:236
  95.2 35.8 %sum_all.1.cross_ref = f32[256,512]{1,0:T(8,128)} custom-call(f32[256,512]{1,0:T(8,128)} %get-tuple-element.4.x_ref), custom_call_target="tpu_custom_call" | custom-call | tf_op jit(solution)/shard_map/sum_all/pallas_call | solution.py:151
  130.9 30.7 %factor.1 = (f32[256,2048]{1,0:T(8,128)}, f32[256,512]{1,0:T(8,128)}) custom-call(f32[256,512]{1,0:T(8,128)} %sum_all.1.cross_ref, f32[256,512]{1,0:T(8,128)} %probes_ref.3, f32[256,2048]{1,0:T(8,128)} %get-tuple-element.5.sk_ref), custom_call_target="tpu_custom_call" | custom-call | tf_op jit(solution)/shard_map/factor/pallas_call | solution.py:64

commit v3 on v2

--- a/solution.py
+++ b/solution.py
@@ -12,29 +12,57 @@
 def mm(a, b, dims):
     return lax.dot_general(a, b, (dims, ((), ())), precision=HI, preferred_element_type=jnp.float32)
 
-def invert_block(block):
+def invert_block(block, group):
     b = block.shape[0]
+    shape = (8, 2 * b)
     rows = lax.broadcasted_iota(jnp.int32, (b, 2 * b), 0)
     cols = lax.broadcasted_iota(jnp.int32, (b, 2 * b), 1)
     eye = (rows + b == cols).astype(jnp.float32)
     m = jnp.concatenate([block, eye[:, b:]], axis=1)
     strips = [m[8 * s:8 * s + 8] for s in range(b // 8)]
-    srow = lax.broadcasted_iota(jnp.int32, (8, 2 * b), 0)
-    for j in range(b - 1):
-        s0, r = divmod(j, 8)
-        pivot = strips[s0][r:r + 1, :]
-        inv = 1.0 / pivot[:, j:j + 1]
-        scaled = pivot * inv
+    srow = lax.broadcasted_iota(jnp.int32, shape, 0)
+    for j in range(0, b, group):
+        s0, r0 = divmod(j, 8)
+        strip = strips[s0]
+        pivots = [jnp.broadcast_to(strip[r0 + r:r0 + r + 1, :], shape) for r in range(group)]
+        corner = [
+            [jnp.broadcast_to(strip[r0 + r:r0 + r + 1, j + c:j + c + 1], shape) for c in range(r + 1)]
+            for r in range(group)
+        ]
+        ratio = [[None] * group for _ in range(group)]
+        scaled = []
+        for r in range(group):
+            inv = 1.0 / corner[r][r]
+            for lo in range(r + 1, group):
+                ratio[lo][r] = corner[lo][r] * inv
+            for lo in range(r + 1, group):
+                for c in range(r + 1, lo + 1):
+                    corner[lo][c] = corner[lo][c] - ratio[lo][r] * corner[c][r]
+                pivots[lo] = pivots[lo] - ratio[lo][r] * pivots[r]
+            scaled.append(pivots[r] * inv)
         for s in range(s0, b // 8):
-            f = strips[s][:, j:j + 1]
+            if s == s0 and r0 + group == 8:
+                new = strips[s]
+            else:
+                held = strips[s]
+                f = []
+                new = held
+                for r in range(group):
+                    fr = jnp.broadcast_to(held[:, j + r:j + r + 1], shape)
+                    for c in range(r):
+                        fr = fr - ratio[r][c] * f[c]
+                    f.append(fr)
+                    new = new - fr * scaled[r]
+                if s == s0:
+                    new = jnp.where(srow >= r0 + group, new, held)
             if s == s0:
-                if r == 7:
-                    continue
-                f = jnp.where(srow[:, :1] > r, f, 0.0)
-            strips[s] = strips[s] - f * scaled
+                for r in range(group):
+                    new = jnp.where(srow == r0 + r, pivots[r], new)
+            strips[s] = new
     m = jnp.concatenate(strips, axis=0)
     d = jnp.sum(jnp.where(rows == cols, m, 0.0), axis=1, keepdims=True)
     return m[:, b:] * lax.rsqrt(d)
+
 
 def factor_kernel(cross_ref, probes_ref, sk_ref, basis_ref, coeffs_ref, aug, winv):
     k = cross_ref.shape[0]
@@ -45,7 +73,7 @@
     aug[:, k:] = (rows == cols).astype(jnp.float32)
     for i in range(k // b):
         lo, hi = i * b, (i + 1) * b
-        w = invert_block(aug[lo:hi, lo:hi])
+        w = invert_block(aug[lo:hi, lo:hi], 8)
         done = mm(w, aug[lo:hi, :], ((1,), (0,)))
         winv[lo:hi, :] = done[:, k:]
         if hi < k:
@@ -68,12 +96,12 @@
         name="factor")(cross, probes, sk)
 
 
-def sum_kernel(n_pts, n_hrs, x_ref, out_ref, got1, part, got2, s1, r1, s2, r2, s3, r3, s4, r4):
+def sum_kernel(n_pts, n_hrs, lanes, cols, x_ref, out_ref, got1, part, got2, s1, r1, s2, r2, s3, r3, s4, r4):
     pts, hrs = lax.axis_index("pts"), lax.axis_index("hrs")
     rows, width = x_ref.shape
     q = rows // n_hrs
-    cols = q * width // (8 * n_pts)
-    per_row = width // cols
+    parts = width // lanes
+    per_row = lanes // cols
 
     def peer_hrs(o):
         return lax.rem(hrs + o, n_hrs)
@@ -81,10 +109,10 @@
     def peer_pts(o):
         return lax.rem(pts + o, n_pts)
 
-    def tile(p):
+    def tile(h, p, first=0):
         return (
-            pl.ds(pl.multiple_of((p // per_row) * 8, 8), 8),
-            pl.ds(pl.multiple_of(lax.rem(p, per_row) * cols, 128), cols),
+            pl.ds(pl.multiple_of(first + (p // per_row) * 8, 8), 8),
+            pl.ds(pl.multiple_of(h * lanes + lax.rem(p, per_row) * cols, 128), cols),
         )
 
     barrier = pltpu.get_barrier_semaphore()
@@ -94,73 +122,88 @@
         pl.semaphore_signal(barrier, inc=1, device_id=(peer_pts(o), hrs), device_id_type=pl.DeviceIdType.MESH)
     pl.semaphore_wait(barrier, n_hrs + n_pts - 2)
 
+    started = []
+
     def send(src, dst, ss, rs, device):
         copy = pltpu.make_async_remote_copy(
             src_ref=src, dst_ref=dst, send_sem=ss, recv_sem=rs,
             device_id=device, device_id_type=pl.DeviceIdType.MESH,
         )
         copy.start()
+        started.append(copy)
         return copy
 
+    def along(h):
+        return pl.ds(h * lanes, lanes)
+
     mine = pl.ds(pl.multiple_of(hrs * q, 8), q)
-    copies = []
-    for o in range(1, n_hrs):
-        t = peer_hrs(o)
-        src = x_ref.at[pl.ds(pl.multiple_of(t * q, 8), q)]
-        copies.append(send(src, got1.at[o - 1], s1.at[o - 1], r1.at[o - 1], (pts, t)))
-    total = x_ref[mine, :]
-    for o, copy in enumerate(copies):
-        copy.wait_recv()
-        total = total + got1[o]
-    part[...] = total
-
-    copies2 = []
-    for o in range(1, n_pts):
-        t = peer_pts(o)
-        copies2.append(send(part.at[tile(t)], got2.at[o - 1], s2.at[o - 1], r2.at[o - 1], (t, hrs)))
-    total = part[tile(pts)]
-    for o, copy in enumerate(copies2):
-        copy.wait_recv()
-        total = total + got2[o]
-    tr, tc = tile(pts)
-    own = (pl.ds(pl.multiple_of(hrs * q + (pts // per_row) * 8, 8), 8), tc)
-    out_ref[own] = total
-
-    copies3 = []
-    for o in range(1, n_pts):
-        t = peer_pts(o)
-        copies3.append(send(out_ref.at[own], out_ref.at[own], s3.at[o - 1], r3.at[o - 1], (t, hrs)))
-    for copy in copies3:
-        copy.wait_recv()
-    copies4 = []
-    for o in range(1, n_hrs):
-        t = peer_hrs(o)
-        copies4.append(send(out_ref.at[mine], out_ref.at[mine], s4.at[o - 1], r4.at[o - 1], (pts, t)))
-    for copy in copies4:
-        copy.wait_recv()
-    for copy in copies + copies2 + copies3 + copies4:
+    first, second, third, fourth = [], [], [], []
+    for h in range(parts):
+        copies = []
+        for o in range(1, n_hrs):
+            t = peer_hrs(o)
+            src = x_ref.at[pl.ds(pl.multiple_of(t * q, 8), q), along(h)]
+            copies.append(send(src, got1.at[h, o - 1], s1.at[h, o - 1], r1.at[h, o - 1], (pts, t)))
+        first.append(copies)
+    for h in range(parts):
+        total = x_ref[mine, along(h)]
+        for o, copy in enumerate(first[h]):
+            copy.wait_recv()
+            total = total + got1[h, o]
+        part[:, along(h)] = total
+        copies = []
+        for o in range(1, n_pts):
+            t = peer_pts(o)
+            copies.append(send(part.at[tile(h, t)], got2.at[h, o - 1], s2.at[h, o - 1], r2.at[h, o - 1], (t, hrs)))
+        second.append(copies)
+    for h in range(parts):
+        total = part[tile(h, pts)]
+        for o, copy in enumerate(second[h]):
+            copy.wait_recv()
+            total = total + got2[h, o]
+        own = tile(h, pts, hrs * q)
+        out_ref[own] = total
+        copies = []
+        for o in range(1, n_pts):
+            t = peer_pts(o)
+            copies.append(send(out_ref.at[own], out_ref.at[own], s3.at[h, o - 1], r3.at[h, o - 1], (t, hrs)))
+        third.append(copies)
+    for h in range(parts):
+        for copy in third[h]:
+            copy.wait_recv()
+        copies = []
+        block = out_ref.at[mine, along(h)]
+        for o in range(1, n_hrs):
+            copies.append(send(block, block, s4.at[h, o - 1], r4.at[h, o - 1], (pts, peer_hrs(o))))
+        fourth.append(copies)
+    for copies in fourth:
+        for copy in copies:
+            copy.wait_recv()
+    for copy in started:
         copy.wait_send()
 
 
-def sum_all(x, n_pts, n_hrs):
+def sum_all(x, n_pts, n_hrs, parts=2):
     rows, width = x.shape
     q = rows // n_hrs
-    cols = q * width // (8 * n_pts)
+    parts = max(1, min(parts, q * width // (8 * 128 * n_pts)))
+    lanes = width // parts
+    cols = q * lanes // (8 * n_pts)
     v = pl.BlockSpec(memory_space=pltpu.VMEM)
     dma = pltpu.SemaphoreType.DMA
     return pl.pallas_call(
-        functools.partial(sum_kernel, n_pts, n_hrs),
+        functools.partial(sum_kernel, n_pts, n_hrs, lanes, cols),
         out_shape=jax.ShapeDtypeStruct(x.shape, jnp.float32),
         in_specs=[v],
         out_specs=v,
         scratch_shapes=[
-            pltpu.VMEM((n_hrs - 1, q, width), jnp.float32),
+            pltpu.VMEM((parts, n_hrs - 1, q, lanes), jnp.float32),
             pltpu.VMEM((q, width), jnp.float32),
-            pltpu.VMEM((n_pts - 1, 8, cols), jnp.float32),
-            dma((n_hrs - 1,)), dma((n_hrs - 1,)),
-            dma((n_pts - 1,)), dma((n_pts - 1,)),
-            dma((n_pts - 1,)), dma((n_pts - 1,)),
-            dma((n_hrs - 1,)), dma((n_hrs - 1,)),
+            pltpu.VMEM((parts, n_pts - 1, 8, cols), jnp.float32),
+            dma((parts, n_hrs - 1)), dma((parts, n_hrs - 1)),
+            dma((parts, n_pts - 1)), dma((parts, n_pts - 1)),
+            dma((parts, n_pts - 1)), dma((parts, n_pts - 1)),
+            dma((parts, n_hrs - 1)), dma((parts, n_hrs - 1)),
         ],
         compiler_params=pltpu.CompilerParams(collective_id=0, has_side_effects=True),
         name="sum_all",

time: 162 us -> 146 us (0.901)
  Pallas kernels: 161 us -> 146 us
    pallas_call x1, Pallas kernels: 30.7 us -> 17.4 us  [finish(): pl.pallas_call(factor_kernel, out_shape=(jax.ShapeDtypeStruct(sk.shape, j...]
    pallas_call x1, Pallas kernels: 35.8 us -> 33.7 us  [sum_all(): pl.pallas_call(functools.partial(sum_kernel, n_pts, n_hrs, lanes, cols),...]
where the time goes in v3:
time: 146 us
  Pallas kernels  146 us (100%)
    pallas_call x1, Pallas kernels, gather(): pl.pallas_call(functools.partial(gather_kernel, n_pts, n_hrs, chunks, n_p...  94.5 us
    pallas_call x1, Pallas kernels, sum_all(): pl.pallas_call(functools.partial(sum_kernel, n_pts, n_hrs, lanes, cols),...  33.7 us
    pallas_call x1, Pallas kernels, finish(): pl.pallas_call(factor_kernel, out_shape=(jax.ShapeDtypeStruct(sk.shape, j...  17.4 us

profile of v3, /device:TPU:0, one launch (start us, length us, event | category | flops | bytes accessed | tf_op | source)
XLA Modules:
  0.0 146.2 jit_solution(8982425043035844869)
XLA Ops:
  0.6 94.5 %gather.1 = (f32[256,2048]{1,0:T(8,128)}, f32[256,512]{1,0:T(8,128)}) custom-call(f32[16,65536]{1,0:T(8,128)} %fields_ref.1, f32[256,512]{1,0:T(8,128)} %probes_ref.3), custom_call_target="tpu_custom_call" | custom-call | tf_op jit(solution)/shard_map/gather/pallas_call | solution.py:279
  95.2 33.7 %sum_all.1.cross_ref = f32[256,512]{1,0:T(8,128)} custom-call(f32[256,512]{1,0:T(8,128)} %get-tuple-element.4.x_ref), custom_call_target="tpu_custom_call" | custom-call | tf_op jit(solution)/shard_map/sum_all/pallas_call | solution.py:194
  128.9 17.4 %factor.1 = (f32[256,2048]{1,0:T(8,128)}, f32[256,512]{1,0:T(8,128)}) custom-call(f32[256,512]{1,0:T(8,128)} %sum_all.1.cross_ref, f32[256,512]{1,0:T(8,128)} %probes_ref.3, f32[256,2048]{1,0:T(8,128)} %get-tuple-element.5.sk_ref), custom_call_target="tpu_custom_call" | custom-call | tf_op jit(solution)/shard_map/factor/pallas_call | solution.py:92
